TPU v7x, 32 devices: a whole 2x2x4 slice. The times are simulated.
32 devices in a mesh: gx: 4 (over x, core), gy: 4 (over z), gz: 2 (over y).
Axes of the slice: x: 2, y: 2, z: 4, core: 2. Of those that a mesh axis runs over, the one named last changes fastest.
Arguments:
- right_side: float32 [16, 16, 8, 4, 256], P('gx', 'gy', 'gz'), may hold values from -80 to 80
- bond_blocks: float32 [13, 4, 4, 16, 16, 8], P(None, None, None, 'gx', 'gy', 'gz'), may hold values from -0.012 to 0.012
- bond_open: int32 [13, 16, 16, 8], P(None, 'gx', 'gy', 'gz'), may hold values 0 or 1
- onsite_blocks: float32 [4, 4, 16, 16, 8], P(None, None, 'gx', 'gy', 'gz'), may hold values from -0.012 to 0.012
- orbital_levels: float32 [4, 16, 16, 8], P(None, 'gx', 'gy', 'gz'), may hold values from 1.3 to 2.6
- column_shift: float32 [256], replicated, may hold values from 0.05 to 1
Outputs:
- solution: float32 [16, 16, 8, 4, 256], P('gx', 'gy', 'gz')
- residual: float32 [16, 16, 8, 4, 256], P('gx', 'gy', 'gz')
All inputs are finite; a program needn't handle non-finite values. No bound on the sum of `bond_open` on one device may be relied on, other than what follows from the above.
Results may differ from a plain program's by a relative error of at most 0.0003.
Values sent between devices are 32-bit elements; how exact they have to be, the bound alone decides.
A program may use at most 192 MiB of HBM per device.

v0:
```python
import jax
import jax.numpy as jnp
from jax import lax
from jax.sharding import PartitionSpec as P

ITERS = 3


half_offsets = [
    (first, second, third)
    for first in (-1, 0, 1)
    for second in (-1, 0, 1)
    for third in (-1, 0, 1)
    if (first, second, third) > (0, 0, 0)
]


def extended_2(cells, sides, width):
    for axis, dim in sides:
        count = lax.axis_size(axis)
        head = lax.slice_in_dim(cells, 0, width, axis=dim)
        tail = lax.slice_in_dim(cells, cells.shape[dim] - width, cells.shape[dim], axis=dim)
        cells = jnp.concatenate(
            [
                lax.ppermute(tail, axis, [(i, (i + 1) % count) for i in range(count)]),
                cells,
                lax.ppermute(head, axis, [((i + 1) % count, i) for i in range(count)]),
            ],
            axis=dim,
        )
    return cells


def shifted(value, axis, by):
    peers = lax.axis_size(axis)
    return lax.ppermute(value, axis, [(i, (i + by) % peers) for i in range(peers)])


def block_apply(blocks, vector, flipped):
    orbitals = vector.shape[3]
    rows = []
    for out_orb in range(orbitals):
        total = None
        for in_orb in range(orbitals):
            factor = blocks[in_orb, out_orb] if flipped else blocks[out_orb, in_orb]
            term = factor[..., None] * vector[:, :, :, in_orb, :]
            total = term if total is None else total + term
        rows.append(total)
    return jnp.stack(rows, axis=3)


def hop(blocks, vector):
    return block_apply(blocks, vector, False)


def hop_back(blocks, vector):
    return block_apply(blocks, vector, True)


def window(extended, offset, counts, base_first):
    return extended[
        base_first + offset[0] : base_first + offset[0] + counts[0],
        1 + offset[1] : 1 + offset[1] + counts[1],
        1 + offset[2] : 1 + offset[2] + counts[2],
    ]


def outer_layer(extended, dim, upper):
    inner = extended.shape[dim] - 2
    if upper:
        return lax.slice_in_dim(extended, inner + 1, inner + 2, axis=dim)
    return lax.slice_in_dim(extended, 0, 1, axis=dim)


def settle(extended, dim, from_lower, from_upper):
    inner = extended.shape[dim] - 2
    core = lax.slice_in_dim(extended, 1, inner + 1, axis=dim)
    pads_lower = [(0, 0)] * extended.ndim
    pads_upper = [(0, 0)] * extended.ndim
    pads_lower[dim] = (0, inner - 1)
    pads_upper[dim] = (inner - 1, 0)
    return core + jnp.pad(from_lower, pads_lower) + jnp.pad(from_upper, pads_upper)


def settle_first(extended, from_lower):
    inner = extended.shape[0] - 1
    core = extended[:inner]
    pads_lower = [(0, 0)] * extended.ndim
    pads_lower[0] = (0, inner - 1)
    return core + jnp.pad(from_lower, pads_lower)


def per_device(right_side, bond_blocks, bond_open, onsite_blocks, orbital_levels, column_shift):
    coupled = bond_blocks * bond_open[:, None, None].astype(jnp.float32)
    onsite_sym = 0.5 * (onsite_blocks + jnp.swapaxes(onsite_blocks, 0, 1))
    atom_levels = jnp.transpose(orbital_levels, (1, 2, 3, 0))
    counts = right_side.shape[:3]

    def operate(vector):
        result = hop(onsite_sym, vector) + (atom_levels[..., None] + column_shift) * vector
        side = extended_2(vector, (("gy", 1), ("gz", 2)), 1)
        following = shifted(side[0:1], "gx", -1)
        extended = jnp.concatenate([side, following], axis=0)
        for bond_index, offset in enumerate(half_offsets):
            result = result + hop(coupled[bond_index], window(extended, offset, counts, 0))
        spilled = jnp.zeros(
            (counts[0] + 1, counts[1] + 2, counts[2] + 2) + vector.shape[3:], jnp.float32
        )
        for bond_index, offset in enumerate(half_offsets):
            placed = (
                (offset[0], 1 - offset[0]),
                (1 + offset[1], 1 - offset[1]),
                (1 + offset[2], 1 - offset[2]),
                (0, 0),
                (0, 0),
            )
            spilled = spilled + jnp.pad(hop_back(coupled[bond_index], vector), placed)
        top_layer = spilled[counts[0] : counts[0] + 1]
        spilled = settle_first(spilled, shifted(top_layer, "gx", 1))
        spilled = settle(
            spilled,
            1,
            shifted(outer_layer(spilled, 1, True), "gy", 1),
            shifted(outer_layer(spilled, 1, False), "gy", -1),
        )
        spilled = settle(
            spilled,
            2,
            shifted(outer_layer(spilled, 2, True), "gz", 1),
            shifted(outer_layer(spilled, 2, False), "gz", -1),
        )
        result = result + spilled
        return result

    def two_products(residual, image):
        return lax.psum(
            (
                jnp.sum(residual * residual, axis=(0, 1, 2, 3)),
                jnp.sum(residual * image, axis=(0, 1, 2, 3)),
            ),
            ("gx", "gy", "gz"),
        )

    solution = jnp.zeros_like(right_side)
    residual = right_side
    image = operate(residual)
    norm_now, product = two_products(residual, image)
    alpha = norm_now / product
    direction = residual
    along = image
    for iteration in range(ITERS):
        solution = solution + alpha * direction
        residual = residual - alpha * along
        if iteration + 1 < ITERS:
            image = operate(residual)
            norm_next, product = two_products(residual, image)
            ratio = norm_next / norm_now
            alpha = norm_next / (product - ratio * norm_next / alpha)
            direction = residual + ratio * direction
            along = image + ratio * along
            norm_now = norm_next
    return (solution, residual)


def solution(mesh):
    placed = (
        P("gx", "gy", "gz", None, None),
        P(None, None, None, "gx", "gy", "gz"),
        P(None, "gx", "gy", "gz"),
        P(None, None, "gx", "gy", "gz"),
        P(None, "gx", "gy", "gz"),
        P(),
    )
    return jax.shard_map(
        per_device,
        mesh=mesh,
        in_specs=placed,
        out_specs=(P("gx", "gy", "gz", None, None), P("gx", "gy", "gz", None, None)),
        check_vma=False,
    )
```

profile of v0, /device:TPU:0, one launch (start us, length us, event | category | flops | bytes accessed | tf_op | source)
XLA Modules:
  0.0 348.6 jit_solution(13338031472730461448)
XLA Ops:
  2.2 3.1 collective-permute-start
  6.3 8.4 %slice_reduce_fusion.12 = (f32[4,4,4,4,4]{4,3,2,1,0:T(4,128)S(1)}, f32[4,4,4,4,4]{4,3,2,1,0:T(4,128)S(1)}, f32[4,4,4,4,4]{4,3,2,1,0:T(4,128)S(1)}, f32[4,4,4,4,4...) fusion(f32[13,4,4,4,4,4]{0,5,4,3,2,1:T(4,128)S(1)} %bitcast.456), kind=kLoop, calls=%fused_computation.212 | loop fusion | bytes 106496 | tf_op jit(solution)/shard_map/slice | solution.py:105
  37.8 8.6 %fusion.36 = f32[5,6,6,4,256]{4,3,2,1,0:T(4,128)S(1)} fusion(f32[4,4,4,1,256]{4,3,2,1,0:T(1,128)S(1)} %get-tuple-element.412, f32[4,4,4,1,256]{4,3,2,1,0:T(1,128)S(1)} %get-tuple-element.411, f32[4,4,4,1,256]{4,3,2,1,0:T(1,128)S(1)} %get-tuple-element.410, f32[4,4,4,1,256]{4,3,2,1,0:T(1,128)S(1)} %get-tuple-element.409, ...), kind=kLoop, calls=%fused_computation.126 | loop fusion | flops 44421120 | bytes 4145152 | tf_op jit(solution)/shard_map/add | solution.py:117
  46.6 2.1 collective-permute-start.1
  55.0 3.7 %collective-permute-start.7 = (f32[4,1,6,4,256]{4,3,2,1,0:T(4,128)S(1)}, f32[4,1,6,4,256]{4,3,2,1,0:T(4,128)S(1)}, u32[]{:S(2)}, u32[]{:S(2)}) collective-permute-start(f32[4,1,6,4,256]{4,3,2,1,0:T(4,128)S(1)} %get-tuple-element.183), channel_id=1, source_target_pairs={{0,6},{2,0},{4,2},{6,4},{1,7},{3,1},{5,3},{7,5},{8,14},{10,8},{12,... | collective-permute-start | bytes 294920 | tf_op jit(solution)/shard_map/ppermute | solution.py:36
  65.2 1.9 collective-permute-start.9
  81.3 4.0 %multiply_reduce_fusion.4 = (f32[256]{0:T(256)S(1)}, f32[256]{0:T(256)S(1)}, f32[4,4,4,4,256]{4,3,2,1,0:T(4,128)S(1)}) fusion(f32[4,4,4,4,256]{4,3,2,1,0:T(4,128)S(1)} %copy-done, f32[4,4,1,4,256]{4,3,2,1,0:T(4,128)S(1)} %collective-permute-done.9, f32[4,4,1,4,256]{4,3,2,1,0:T(4,128)S(1)} %collective-permute-done.8, f32[4,4,6,4,256]{4,3,2,1,0:T(4,128)S(1)} %fusion.62, ...), kind=kLoop, calls=%fused_computation.291 | loop fusion | flops 4259328 | bytes 4591616 | tf_op jit(solution)/shard_map/reduce_sum | solution.py:139
  85.2 39.4 %all-reduce.56 = (f32[256]{0:T(256)S(1)}, f32[256]{0:T(256)S(1)}) all-reduce(f32[256]{0:T(256)S(1)} %get-tuple-element.20, f32[256]{0:T(256)S(1)} %get-tuple-element.19), channel_id=1, replica_groups=mesh['gx'=4,'gy'=4,'gz'=2] {'gx','gy','gz'}, use_global_device_ids=true, to_apply=%region_1.2 | all-reduce | flops 512 | bytes 4096 | tf_op jit(solution)/shard_map/psum | solution.py:136
  149.8 8.6 %fusion.24 = f32[5,6,6,4,256]{4,3,2,1,0:T(4,128)S(1)} fusion(f32[4,4,4,1,256]{4,3,2,1,0:T(1,128)S(1)} %multiply_add_fusion.110, f32[4,4,4,1,256]{4,3,2,1,0:T(1,128)S(1)} %get-tuple-element.343, f32[4,4,4,1,256]{4,3,2,1,0:T(1,128)S(1)} %get-tuple-element.342, f32[4,4,4,1,256]{4,3,2,1,0:T(1,128)S(1)} %get-tuple-element.341, ...), kind=kLoop, calls=%fused_computation.75 | loop fusion | flops 44421120 | bytes 4145152 | tf_op jit(solution)/shard_map/add | solution.py:117
  159.0 2.3 collective-permute-start.12
  162.4 2.1 collective-permute-done.12
  170.3 3.3 collective-permute-start.17
  186.2 2.4 collective-permute-start.19
  189.4 2.1 collective-permute-done.19
  192.9 4.0 %multiply_reduce_fusion.2 = (f32[256]{0:T(256)S(1)}, f32[256]{0:T(256)S(1)}, f32[4,4,4,4,256]{4,3,2,1,0:T(4,128)S(1)}) fusion(f32[4,4,4,4,256]{4,3,2,1,0:T(4,128)S(1)} %multiply_subtract_fusion.2, f32[4,4,1,4,256]{4,3,2,1,0:T(4,128)S(1)} %collective-permute-done.19, f32[4,4,1,4,256]{4,3,2,1,0:T(4,128)S(1)} %collective-permute-done.18, ...), kind=kLoop, calls=%fused_computation.288 | loop fusion | flops 4259328 | bytes 4591616 | tf_op jit(solution)/shard_map/reduce_sum | solution.py:139
  196.9 39.3 %all-reduce.55 = (f32[256]{0:T(256)S(1)}, f32[256]{0:T(256)S(1)}) all-reduce(f32[256]{0:T(256)S(1)} %get-tuple-element.18, f32[256]{0:T(256)S(1)} %get-tuple-element.17), channel_id=1, replica_groups=mesh['gx'=4,'gy'=4,'gz'=2] {'gx','gy','gz'}, use_global_device_ids=true, to_apply=%region_5.6 | all-reduce | flops 512 | bytes 4096 | tf_op jit(solution)/shard_map/psum | solution.py:136
  261.2 8.6 %fusion.12 = f32[5,6,6,4,256]{4,3,2,1,0:T(4,128)S(1)} fusion(f32[4,4,4,1,256]{4,3,2,1,0:T(1,128)S(1)} %multiply_add_fusion.2, f32[4,4,4,1,256]{4,3,2,1,0:T(1,128)S(1)} %get-tuple-element.281, f32[4,4,4,1,256]{4,3,2,1,0:T(1,128)S(1)} %get-tuple-element.280, f32[4,4,4,1,256]{4,3,2,1,0:T(1,128)S(1)} %get-tuple-element.279, ...), kind=kLoop, calls=%fused_computation.24 | loop fusion | flops 44421120 | bytes 4145152 | tf_op jit(solution)/shard_map/add | solution.py:117
  270.2 2.3 collective-permute-start.22
  273.6 2.1 collective-permute-done.22
  281.5 3.2 collective-permute-start.27
  297.4 2.4 collective-permute-start.29
  300.6 2.1 collective-permute-done.29
  304.0 4.0 %multiply_reduce_fusion = (f32[256]{0:T(256)S(1)}, f32[256]{0:T(256)S(1)}, f32[4,4,4,4,256]{4,3,2,1,0:T(4,128)S(1)}) fusion(f32[4,4,4,4,256]{4,3,2,1,0:T(4,128)S(1)} %multiply_subtract_fusion.1, f32[4,4,1,4,256]{4,3,2,1,0:T(4,128)S(1)} %collective-permute-done.29, f32[4,4,1,4,256]{4,3,2,1,0:T(4,128)S(1)} %collective-permute-done.28, ...), kind=kLoop, calls=%fused_computation.284 | loop fusion | flops 4259328 | bytes 4591616 | tf_op jit(solution)/shard_map/reduce_sum | solution.py:139
  308.0 39.1 %all-reduce.54 = (f32[256]{0:T(256)S(1)}, f32[256]{0:T(256)S(1)}) all-reduce(f32[256]{0:T(256)S(1)} %get-tuple-element.16, f32[256]{0:T(256)S(1)} %get-tuple-element.15), channel_id=1, replica_groups=mesh['gx'=4,'gy'=4,'gz'=2] {'gx','gy','gz'}, use_global_device_ids=true, to_apply=%region_9.10 | all-reduce | flops 512 | bytes 4096 | tf_op jit(solution)/shard_map/psum | solution.py:136
  (338 shorter events, 146.1 us)
Async XLA Ops:
  2.2 46.7 %collective-permute-start = (f32[4,1,4,4,256]{4,3,2,1,0:T(4,128)}, f32[4,1,4,4,256]{4,3,2,1,0:T(4,128)}, u32[]{:S(2)}, u32[]{:S(2)}) collective-permute-start(f32[4,1,4,4,256]{4,3,2,1,0:T(4,128)} %get-tuple-element.364), channel_id=1, source_target_pairs={{0,2},{2,4},{4,6},{6,0},{1,3},{3,5},{5,7},{7,1},{8,10},{10,12},{12... | collective-permute-start | bytes 196616 | tf_op jit(solution)/shard_map/ppermute | solution.py:25
  46.5 8.3 %collective-permute-start.5 = (f32[1,6,6,4,256]{4,3,2,1,0:T(4,128)S(1)}, f32[1,6,6,4,256]{4,3,2,1,0:T(4,128)S(1)}, u32[]{:S(2)}, u32[]{:S(2)}) collective-permute-start(f32[1,6,6,4,256]{4,3,2,1,0:T(4,128)S(1)} %slice.1794), channel_id=1, source_target_pairs={{0,8},{8,16},{16,24},{24,0},{1,9},{9,17},{17,25},{25,1},{2,10},{10... | collective-permute-start | bytes 442376 | tf_op jit(solution)/shard_map/ppermute | solution.py:36
  51.3 7.4 %collective-permute-start.2 = (f32[4,6,1,4,256]{4,3,2,1,0:T(4,128)S(1)}, f32[4,6,1,4,256]{4,3,2,1,0:T(4,128)S(1)}, u32[]{:S(2)}, u32[]{:S(2)}) collective-permute-start(f32[4,6,1,4,256]{4,3,2,1,0:T(4,128)S(1)} %get-tuple-element.209), channel_id=1, source_target_pairs={{1,0},{0,1},{3,2},{2,3},{5,4},{4,5},{7,6},{6,7},{9,8},{8,9},{11,10... | collective-permute-start | bytes 294920 | tf_op jit(solution)/shard_map/ppermute | solution.py:27
  52.9 5.9 %collective-permute-start.3 = (f32[4,6,1,4,256]{4,3,2,1,0:T(4,128)S(1)}, f32[4,6,1,4,256]{4,3,2,1,0:T(4,128)S(1)}, u32[]{:S(2)}, u32[]{:S(2)}) collective-permute-start(f32[4,6,1,4,256]{4,3,2,1,0:T(4,128)S(1)} %get-tuple-element.208), channel_id=1, source_target_pairs={{0,1},{1,0},{2,3},{3,2},{4,5},{5,4},{6,7},{7,6},{8,9},{9,8},{10,11... | collective-permute-start | bytes 294920 | tf_op jit(solution)/shard_map/ppermute | solution.py:25
  55.0 9.0 %collective-permute-start.7 = (f32[4,1,6,4,256]{4,3,2,1,0:T(4,128)S(1)}, f32[4,1,6,4,256]{4,3,2,1,0:T(4,128)S(1)}, u32[]{:S(2)}, u32[]{:S(2)}) collective-permute-start(f32[4,1,6,4,256]{4,3,2,1,0:T(4,128)S(1)} %get-tuple-element.183), channel_id=1, source_target_pairs={{0,6},{2,0},{4,2},{6,4},{1,7},{3,1},{5,3},{7,5},{8,14},{10,8},{12,... | collective-permute-start | bytes 294920 | tf_op jit(solution)/shard_map/ppermute | solution.py:36
  58.7 6.4 %collective-permute-start.6 = (f32[4,1,6,4,256]{4,3,2,1,0:T(4,128)S(1)}, f32[4,1,6,4,256]{4,3,2,1,0:T(4,128)S(1)}, u32[]{:S(2)}, u32[]{:S(2)}) collective-permute-start(f32[4,1,6,4,256]{4,3,2,1,0:T(4,128)S(1)} %get-tuple-element.182), channel_id=1, source_target_pairs={{0,2},{2,4},{4,6},{6,0},{1,3},{3,5},{5,7},{7,1},{8,10},{10,12},{12... | collective-permute-start | bytes 294920 | tf_op jit(solution)/shard_map/ppermute | solution.py:36
  58.8 8.5 %collective-permute-start.4 = (f32[1,6,6,4,256]{4,3,2,1,0:T(4,128)S(1)}, f32[1,6,6,4,256]{4,3,2,1,0:T(4,128)S(1)}, u32[]{:S(2)}, u32[]{:S(2)}) collective-permute-start(f32[1,6,6,4,256]{4,3,2,1,0:T(4,128)S(1)} %pad_maximum_fusion.13), channel_id=1, source_target_pairs={{0,24},{8,0},{16,8},{24,16},{1,25},{9,1},{17,9},{25,17},{2,26},{10... | collective-permute-start | bytes 442376 | tf_op jit(solution)/shard_map/ppermute | solution.py:36
  65.2 15.3 %collective-permute-start.9 = (f32[4,4,1,4,256]{4,3,2,1,0:T(4,128)S(1)}, f32[4,4,1,4,256]{4,3,2,1,0:T(4,128)S(1)}, u32[]{:S(2)}, u32[]{:S(2)}) collective-permute-start(f32[4,4,1,4,256]{4,3,2,1,0:T(4,128)S(1)} %get-tuple-element.211), channel_id=1, source_target_pairs={{0,1},{1,0},{2,3},{3,2},{4,5},{5,4},{6,7},{7,6},{8,9},{9,8},{10,11... | collective-permute-start | bytes 196616 | tf_op jit(solution)/shard_map/ppermute | solution.py:36
  67.2 13.4 %collective-permute-start.8 = (f32[4,4,1,4,256]{4,3,2,1,0:T(4,128)S(1)}, f32[4,4,1,4,256]{4,3,2,1,0:T(4,128)S(1)}, u32[]{:S(2)}, u32[]{:S(2)}) collective-permute-start(f32[4,4,1,4,256]{4,3,2,1,0:T(4,128)S(1)} %get-tuple-element.210), channel_id=1, source_target_pairs={{0,1},{1,0},{2,3},{3,2},{4,5},{5,4},{6,7},{7,6},{8,9},{9,8},{10,11... | collective-permute-start | bytes 196616 | tf_op jit(solution)/shard_map/ppermute | solution.py:36
  146.6 12.4 %collective-permute-start.10 = (f32[4,1,4,4,256]{4,3,2,1,0:T(4,128)S(1)}, f32[4,1,4,4,256]{4,3,2,1,0:T(4,128)S(1)}, u32[]{:S(2)}, u32[]{:S(2)}) collective-permute-start(f32[4,1,4,4,256]{4,3,2,1,0:T(4,128)S(1)} %get-tuple-element.296), channel_id=1, source_target_pairs={{0,2},{2,4},{4,6},{6,0},{1,3},{3,5},{5,7},{7,1},{8,10},{10,12},{12... | collective-permute-start | bytes 196616 | tf_op jit(solution)/shard_map/ppermute | solution.py:25
  158.4 11.7 %collective-permute-start.15 = (f32[1,6,6,4,256]{4,3,2,1,0:T(4,128)S(1)}, f32[1,6,6,4,256]{4,3,2,1,0:T(4,128)S(1)}, u32[]{:S(2)}, u32[]{:S(2)}) collective-permute-start(f32[1,6,6,4,256]{4,3,2,1,0:T(4,128)S(1)} %slice.1852), channel_id=1, source_target_pairs={{0,8},{8,16},{16,24},{24,0},{1,9},{9,17},{17,25},{25,1},{2,10},{10... | collective-permute-start | bytes 442376 | tf_op jit(solution)/shard_map/ppermute | solution.py:36
  159.0 5.5 %collective-permute-start.12 = (f32[4,6,1,4,256]{4,3,2,1,0:T(4,128)S(1)}, f32[4,6,1,4,256]{4,3,2,1,0:T(4,128)S(1)}, u32[]{:S(2)}, u32[]{:S(2)}) collective-permute-start(f32[4,6,1,4,256]{4,3,2,1,0:T(4,128)S(1)} %get-tuple-element.205), channel_id=1, source_target_pairs={{1,0},{0,1},{3,2},{2,3},{5,4},{4,5},{7,6},{6,7},{9,8},{8,9},{11,10... | collective-permute-start | bytes 294920 | tf_op jit(solution)/shard_map/ppermute | solution.py:27
  161.3 5.7 %collective-permute-start.13 = (f32[4,6,1,4,256]{4,3,2,1,0:T(4,128)S(1)}, f32[4,6,1,4,256]{4,3,2,1,0:T(4,128)S(1)}, u32[]{:S(2)}, u32[]{:S(2)}) collective-permute-start(f32[4,6,1,4,256]{4,3,2,1,0:T(4,128)S(1)} %get-tuple-element.204), channel_id=1, source_target_pairs={{0,1},{1,0},{2,3},{3,2},{4,5},{5,4},{6,7},{7,6},{8,9},{9,8},{10,11... | collective-permute-start | bytes 294920 | tf_op jit(solution)/shard_map/ppermute | solution.py:25
  167.0 6.6 %collective-permute-start.14 = (f32[1,6,6,4,256]{4,3,2,1,0:T(4,128)S(1)}, f32[1,6,6,4,256]{4,3,2,1,0:T(4,128)S(1)}, u32[]{:S(2)}, u32[]{:S(2)}) collective-permute-start(f32[1,6,6,4,256]{4,3,2,1,0:T(4,128)S(1)} %pad_maximum_fusion.9), channel_id=1, source_target_pairs={{0,24},{8,0},{16,8},{24,16},{1,25},{9,1},{17,9},{25,17},{2,26},{10... | collective-permute-start | bytes 442376 | tf_op jit(solution)/shard_map/ppermute | solution.py:36
  170.3 15.8 %collective-permute-start.17 = (f32[4,1,6,4,256]{4,3,2,1,0:T(4,128)S(1)}, f32[4,1,6,4,256]{4,3,2,1,0:T(4,128)S(1)}, u32[]{:S(2)}, u32[]{:S(2)}) collective-permute-start(f32[4,1,6,4,256]{4,3,2,1,0:T(4,128)S(1)} %get-tuple-element.181), channel_id=1, source_target_pairs={{0,6},{2,0},{4,2},{6,4},{1,7},{3,1},{5,3},{7,5},{8,14},{10,8},{12,... | collective-permute-start | bytes 294920 | tf_op jit(solution)/shard_map/ppermute | solution.py:36
  173.6 12.5 %collective-permute-start.16 = (f32[4,1,6,4,256]{4,3,2,1,0:T(4,128)S(1)}, f32[4,1,6,4,256]{4,3,2,1,0:T(4,128)S(1)}, u32[]{:S(2)}, u32[]{:S(2)}) collective-permute-start(f32[4,1,6,4,256]{4,3,2,1,0:T(4,128)S(1)} %get-tuple-element.180), channel_id=1, source_target_pairs={{0,2},{2,4},{4,6},{6,0},{1,3},{3,5},{5,7},{7,1},{8,10},{10,12},{12... | collective-permute-start | bytes 294920 | tf_op jit(solution)/shard_map/ppermute | solution.py:36
  186.2 5.3 %collective-permute-start.19 = (f32[4,4,1,4,256]{4,3,2,1,0:T(4,128)S(1)}, f32[4,4,1,4,256]{4,3,2,1,0:T(4,128)S(1)}, u32[]{:S(2)}, u32[]{:S(2)}) collective-permute-start(f32[4,4,1,4,256]{4,3,2,1,0:T(4,128)S(1)} %get-tuple-element.207), channel_id=1, source_target_pairs={{0,1},{1,0},{2,3},{3,2},{4,5},{5,4},{6,7},{7,6},{8,9},{9,8},{10,11... | collective-permute-start | bytes 196616 | tf_op jit(solution)/shard_map/ppermute | solution.py:36
  257.9 12.2 %collective-permute-start.20 = (f32[4,1,4,4,256]{4,3,2,1,0:T(4,128)S(1)}, f32[4,1,4,4,256]{4,3,2,1,0:T(4,128)S(1)}, u32[]{:S(2)}, u32[]{:S(2)}) collective-permute-start(f32[4,1,4,4,256]{4,3,2,1,0:T(4,128)S(1)} %get-tuple-element.234), channel_id=1, source_target_pairs={{0,2},{2,4},{4,6},{6,0},{1,3},{3,5},{5,7},{7,1},{8,10},{10,12},{12... | collective-permute-start | bytes 196616 | tf_op jit(solution)/shard_map/ppermute | solution.py:25
  269.8 11.5 %collective-permute-start.25 = (f32[1,6,6,4,256]{4,3,2,1,0:T(4,128)S(1)}, f32[1,6,6,4,256]{4,3,2,1,0:T(4,128)S(1)}, u32[]{:S(2)}, u32[]{:S(2)}) collective-permute-start(f32[1,6,6,4,256]{4,3,2,1,0:T(4,128)S(1)} %slice.1910), channel_id=1, source_target_pairs={{0,8},{8,16},{16,24},{24,0},{1,9},{9,17},{17,25},{25,1},{2,10},{10... | collective-permute-start | bytes 442376 | tf_op jit(solution)/shard_map/ppermute | solution.py:36
  270.2 5.5 %collective-permute-start.22 = (f32[4,6,1,4,256]{4,3,2,1,0:T(4,128)S(1)}, f32[4,6,1,4,256]{4,3,2,1,0:T(4,128)S(1)}, u32[]{:S(2)}, u32[]{:S(2)}) collective-permute-start(f32[4,6,1,4,256]{4,3,2,1,0:T(4,128)S(1)} %get-tuple-element.201), channel_id=1, source_target_pairs={{1,0},{0,1},{3,2},{2,3},{5,4},{4,5},{7,6},{6,7},{9,8},{8,9},{11,10... | collective-permute-start | bytes 294920 | tf_op jit(solution)/shard_map/ppermute | solution.py:27
  272.5 5.7 %collective-permute-start.23 = (f32[4,6,1,4,256]{4,3,2,1,0:T(4,128)S(1)}, f32[4,6,1,4,256]{4,3,2,1,0:T(4,128)S(1)}, u32[]{:S(2)}, u32[]{:S(2)}) collective-permute-start(f32[4,6,1,4,256]{4,3,2,1,0:T(4,128)S(1)} %get-tuple-element.200), channel_id=1, source_target_pairs={{0,1},{1,0},{2,3},{3,2},{4,5},{5,4},{6,7},{7,6},{8,9},{9,8},{10,11... | collective-permute-start | bytes 294920 | tf_op jit(solution)/shard_map/ppermute | solution.py:25
  278.2 6.5 %collective-permute-start.24 = (f32[1,6,6,4,256]{4,3,2,1,0:T(4,128)S(1)}, f32[1,6,6,4,256]{4,3,2,1,0:T(4,128)S(1)}, u32[]{:S(2)}, u32[]{:S(2)}) collective-permute-start(f32[1,6,6,4,256]{4,3,2,1,0:T(4,128)S(1)} %pad_maximum_fusion.5), channel_id=1, source_target_pairs={{0,24},{8,0},{16,8},{24,16},{1,25},{9,1},{17,9},{25,17},{2,26},{10... | collective-permute-start | bytes 442376 | tf_op jit(solution)/shard_map/ppermute | solution.py:36
  281.5 15.8 %collective-permute-start.27 = (f32[4,1,6,4,256]{4,3,2,1,0:T(4,128)S(1)}, f32[4,1,6,4,256]{4,3,2,1,0:T(4,128)S(1)}, u32[]{:S(2)}, u32[]{:S(2)}) collective-permute-start(f32[4,1,6,4,256]{4,3,2,1,0:T(4,128)S(1)} %get-tuple-element.179), channel_id=1, source_target_pairs={{0,6},{2,0},{4,2},{6,4},{1,7},{3,1},{5,3},{7,5},{8,14},{10,8},{12,... | collective-permute-start | bytes 294920 | tf_op jit(solution)/shard_map/ppermute | solution.py:36
  284.8 12.5 %collective-permute-start.26 = (f32[4,1,6,4,256]{4,3,2,1,0:T(4,128)S(1)}, f32[4,1,6,4,256]{4,3,2,1,0:T(4,128)S(1)}, u32[]{:S(2)}, u32[]{:S(2)}) collective-permute-start(f32[4,1,6,4,256]{4,3,2,1,0:T(4,128)S(1)} %get-tuple-element.178), channel_id=1, source_target_pairs={{0,2},{2,4},{4,6},{6,0},{1,3},{3,5},{5,7},{7,1},{8,10},{10,12},{12... | collective-permute-start | bytes 294920 | tf_op jit(solution)/shard_map/ppermute | solution.py:36
  (43 other events, 367.2 us)
where the time goes:
time: 355 us; the launch traced here: 349 us
  other arithmetic  159 us (45%)
  blocking collectives  118 us (33%)
  starting transfers between devices  37.1 us (10%)
  waiting for transfers between devices  17.9 us (5%)
  local copies, waits for them, and re-layouts  13.9 us (4%)
    psum x3, blocking collectives, two_products(): lax.psum((jnp.sum(residual * residual, axis=(0, 1, 2, 3)), jnp.sum(residu...  118 us
    add x162, other arithmetic, block_apply(): total = term if total is None else total + term  117 us
    add x3, other arithmetic, operate(): spilled = spilled + jnp.pad(hop_back(coupled[bond_index], vector), placed)  25.9 us
    ppermute x18, starting transfers between devices, shifted(): lax.ppermute(value, axis, [(i, (i + by) % peers) for i in range(peers)])  20.5 us
    reduce_sum x3, other arithmetic, two_products(): jnp.sum(residual * image, axis=(0, 1, 2, 3))  11.9 us
    ppermute x6, starting transfers between devices, extended_2(): lax.ppermute(head, axis, [((i + 1) % count, i) for i in range(count)])  11.6 us
    ppermute x6, waiting for transfers between devices, extended_2(): lax.ppermute(head, axis, [((i + 1) % count, i) for i in range(count)])  9.28 us
    slice x1, local copies, waits for them, and re-layouts, operate(): coupled[bond_index]  8.42 us
  transfers between devices with their start and end apart: 30, of which 12 were waited for; matrix products, arithmetic and copies ran while one was open for 33% of the time, Pallas kernels for 0%

commit v1 on v0

v1 whole, which is shorter than its diff:
```python
import functools
import itertools

import jax
import jax.numpy as jnp
import numpy as np
from jax import lax
from jax.experimental import pallas as pl
from jax.experimental.pallas import tpu as pltpu
from jax.sharding import PartitionSpec as P

ITERS = 3
LANES = 128
HALF = 64
ROWS = 8
AXES = ("gx", "gy", "gz")
MESH = pl.DeviceIdType.MESH

half_offsets = [o for o in itertools.product((-1, 0, 1), repeat=3) if o > (0, 0, 0)]
directions = [d for d in itertools.product((-1, 0, 1), repeat=3) if d != (0, 0, 0)]


def up(value, step):
    return -(-value // step) * step


class Plan:
    def __init__(self, block, orbitals, peers_along):
        self.block, self.orb = block, orbitals
        self.own = block[0] * block[1] * block[2] * orbitals
        self.base = 4 * max(block) + 8
        codes = [self.code(p) for p in itertools.product(*map(range, block)) for _ in range(orbitals)]
        self.regions, at = [], 0
        for d in directions:
            here = [{0: range(n), 1: [n], -1: [-1]}[s] for s, n in zip(d, block)]
            there = [{0: range(n), 1: [0], -1: [n - 1]}[s] for s, n in zip(d, block)]
            positions = list(itertools.product(*here))
            codes += [self.code(p) for p in positions for _ in range(orbitals)]
            pieces = []
            for slot, p in enumerate(itertools.product(*there)):
                row = ((p[0] * block[1] + p[1]) * block[2] + p[2]) * orbitals
                target = at + slot * orbitals
                if pieces and pieces[-1][0] + pieces[-1][2] == row:
                    pieces[-1][2] += orbitals
                else:
                    pieces.append([row, target, orbitals])
            rows = len(positions) * orbitals
            size = up(rows, 8)
            codes += [10**6] * (size - rows)
            self.regions.append((d, at, rows, size, pieces))
            at += size
        self.halo = at
        self.ext = up(self.own + at, LANES)
        self.halo_all = self.ext - self.own
        codes += [10**6] * (self.ext - len(codes))
        self.codes = np.array(codes, np.float32)
        nx, ny, nz = peers_along
        self.peers_along = peers_along
        self.first = [(a, 0, c) for a in range(nx) for c in range(nz) if (a, c) != (0, 0)]
        self.second = [(0, b, 0) for b in range(1, ny)]
        greet = {tuple(s % n for s, n in zip(d, peers_along)) for d in directions}
        self.greet = sorted(greet | set(self.first) | set(self.second))

    def code(self, position):
        return (position[0] * self.base + position[1]) * self.base + position[2]


def kernel(plan, rs_ref, w_ref, shift_ref, code_ref, spread_ref, sol_ref, res_ref,
           send0, recv0, sends, recvs, ext, along, a_hi, a_lo, part1, got1, part2, got2,
           hs_sem, hr_sem, s1_sem, r1_sem, s2_sem, r2_sem):
    cols = rs_ref.shape[1]
    own, orb = plan.own, plan.orb
    halo, halo_all, full = plan.halo, plan.halo_all, plan.ext
    bonds = len(half_offsets)

    def at(relative):
        return tuple(
            lax.rem(lax.axis_index(name) + (s % n), n)
            for name, s, n in zip(AXES, relative, plan.peers_along)
        )

    barrier = pltpu.get_barrier_semaphore()
    for relative in plan.greet:
        pl.semaphore_signal(barrier, inc=1, device_id=at(relative), device_id_type=MESH)

    def pack(value, send_ref, lane):
        width = value.shape[1]
        for d, start, rows, size, pieces in plan.regions:
            parts = [value[source:source + count, :] for source, target, count in pieces]
            if size > rows:
                parts.append(jnp.zeros((size - rows, width), jnp.float32))
            whole = parts[0] if len(parts) == 1 else jnp.concatenate(parts, axis=0)
            send_ref[start:start + size, lane:lane + width] = whole

    pack(rs_ref[...], send0, 0)
    pack(w_ref[...], send0, cols)
    pl.semaphore_wait(barrier, len(plan.greet))

    def halo_copies(turn, source, target):
        copies = []
        for m, (d, start, rows, size, pieces) in enumerate(plan.regions):
            copies.append(pltpu.make_async_remote_copy(
                src_ref=source.at[pl.ds(start, size)],
                dst_ref=target.at[pl.ds(start, size)],
                send_sem=hs_sem.at[turn, m],
                recv_sem=hr_sem.at[turn, m],
                device_id=at(tuple(-s for s in d)),
                device_id_type=MESH,
            ))
        return copies

    flight = halo_copies(0, send0, recv0)
    for copy in flight:
        copy.start()

    code_lane = code_ref[...][0:1, :]
    code_row = jnp.transpose(jnp.broadcast_to(code_lane, (LANES, full)))[:, 0:1]
    steps = [float(plan.code(o)) for o in half_offsets]
    lane_of = lax.broadcasted_iota(jnp.int32, (LANES, LANES), 1)

    def spread(rows_of_w):
        high = rows_of_w.astype(jnp.bfloat16).astype(jnp.float32)
        both = jnp.where(lane_of < HALF, high, rows_of_w - high).astype(jnp.bfloat16)
        return jnp.dot(both, spread_ref[...], preferred_element_type=jnp.float32)

    def placed(tiles, row_codes, lane_codes, sign, count):
        width = lane_codes.shape[1]
        blocks = []
        for g in range(0, width, LANES):
            gap = (lane_codes[:, g:g + LANES] - row_codes) * sign
            total = jnp.zeros((LANES, LANES), jnp.float32)
            for k in range(count):
                step = steps[k] if k < bonds else 0.0
                total = jnp.where(gap == step, tiles[:, k * LANES:(k + 1) * LANES], total)
            blocks.append(total)
        return jnp.concatenate(blocks, axis=1)

    ext[0:own, :] = rs_ref[...]
    forward = []
    backward = []
    for b in range(0, own, LANES):
        tiles = spread(w_ref[b:b + LANES, :])
        forward.append(placed(tiles, code_row[b:b + LANES], code_lane, 1.0, bonds + 1))
        backward.append(placed(tiles, code_row[b:b + LANES], code_lane[:, 0:own], 1.0, bonds))
    for copy in flight:
        copy.wait_recv()
    ext[own:own + halo, :] = recv0[0:halo, 0:cols]
    if own + halo < full:
        ext[own + halo:full, :] = jnp.zeros((full - own - halo, cols), jnp.float32)
        recv0[halo:halo_all, :] = jnp.zeros((halo_all - halo, cols + LANES), jnp.float32)
    for b in range(0, halo_all, LANES):
        tiles = spread(recv0[b:b + LANES, cols:cols + LANES])
        rows = code_row[own + b:own + b + LANES]
        backward.append(placed(tiles, rows, code_lane[:, 0:own], 1.0, bonds))
    for b in range(0, own, LANES):
        for g in range(0, full, LANES):
            block = forward[b // LANES][:, g:g + LANES] + jnp.transpose(backward[g // LANES][:, b:b + LANES])
            high = block.astype(jnp.bfloat16)
            a_hi[b:b + LANES, g:g + LANES] = high
            a_lo[b:b + LANES, g:g + LANES] = (block - high.astype(jnp.float32)).astype(jnp.bfloat16)

    diagonal = w_ref[...][:, (bonds + 1) * orb:(bonds + 1) * orb + 1] + shift_ref[...]

    def operate():
        vector = ext[...]
        high = vector.astype(jnp.bfloat16)
        low = (vector - high.astype(jnp.float32)).astype(jnp.bfloat16)
        total = jnp.dot(a_hi[...], low, preferred_element_type=jnp.float32)
        total = total + jnp.dot(a_lo[...], high, preferred_element_type=jnp.float32)
        total = total + jnp.dot(a_hi[...], high, preferred_element_type=jnp.float32)
        return total + diagonal * ext[0:own, :]

    pending = list(flight)

    def group(turn, members, source, target, send_sem, recv_sem):
        copies = []
        for m, relative in enumerate(members):
            copies.append(pltpu.make_async_remote_copy(
                src_ref=source.at[turn],
                dst_ref=target.at[turn, m],
                send_sem=send_sem.at[turn, m],
                recv_sem=recv_sem.at[turn, m],
                device_id=at(relative),
                device_id_type=MESH,
            ))
        for copy in copies:
            copy.start()
        pending.extend(copies)
        return copies

    for turn in range(ITERS):
        image = operate()
        mine = ext[0:own, :]
        part1[turn] = jnp.concatenate([
            jnp.sum(mine * mine, axis=0, keepdims=True),
            jnp.sum(mine * image, axis=0, keepdims=True),
            jnp.zeros((ROWS - 2, cols), jnp.float32),
        ], axis=0)
        sums = group(turn, plan.first, part1, got1, s1_sem, r1_sem)
        last = turn + 1 == ITERS
        if turn == 0:
            along[0:own, :] = image
        else:
            res_ref[...] = image
        if not last:
            pack(image, sends.at[turn], 0)
            flight = halo_copies(turn + 1, sends.at[turn], recvs.at[turn])
            for copy in flight:
                copy.start()
            pending.extend(flight)
        total = part1[turn]
        for m, copy in enumerate(sums):
            copy.wait_recv()
            total = total + got1[turn, m]
        part2[turn] = total
        sums = group(turn, plan.second, part2, got2, s2_sem, r2_sem)
        for m, copy in enumerate(sums):
            copy.wait_recv()
            total = total + got2[turn, m]
        norm, product = total[0:1], total[1:2]
        if turn == 0:
            alpha = norm / product
            direction = mine
            sol_ref[...] = alpha * mine
        else:
            ratio = norm / norm_before
            alpha = norm / (product - ratio * norm / alpha)
            direction = mine + ratio * direction
            sol_ref[...] = sol_ref[...] + alpha * direction
            along[0:own, :] = res_ref[...] + ratio * along[0:own, :]
        norm_before = norm
        if last:
            res_ref[...] = mine - alpha * along[0:own, :]
        else:
            ext[0:own, :] = mine - alpha * along[0:own, :]
            for copy in flight:
                copy.wait_recv()
            edge = recvs[turn, 0:halo, :]
            if turn > 0:
                edge = edge + ratio * along[own:own + halo, :]
            along[own:own + halo, :] = edge
            ext[own:own + halo, :] = ext[own:own + halo, :] - alpha * edge
    for copy in pending:
        copy.wait_send()


def per_device(peers_along, right_side, bond_blocks, bond_open, onsite_blocks, orbital_levels, column_shift):
    block, orb, cols = right_side.shape[:3], right_side.shape[3], right_side.shape[4]
    plan = Plan(block, orb, peers_along)
    own, bonds = plan.own, len(half_offsets)
    coupled = bond_blocks * bond_open[:, None, None].astype(jnp.float32)
    onsite_sym = 0.5 * (onsite_blocks + jnp.swapaxes(onsite_blocks, 0, 1))
    atoms = own // orb
    lines = jnp.concatenate([coupled, onsite_sym[None]], axis=0).reshape(bonds + 1, orb, orb, atoms)
    lines = jnp.transpose(lines, (3, 1, 0, 2)).reshape(own, (bonds + 1) * orb)
    levels = jnp.transpose(orbital_levels.reshape(orb, atoms)).reshape(own, 1)
    lines = jnp.concatenate([lines, levels, jnp.zeros((own, HALF - lines.shape[1] - 1), jnp.float32)], axis=1)
    lines = jnp.concatenate([lines, lines], axis=1)

    count = bonds + 1
    spread = np.zeros((2, HALF, count, LANES), np.float32)
    for k in range(count):
        for t in range(LANES):
            spread[:, k * orb + t % orb, k, t] = 1.0
    spread = jnp.asarray(spread.reshape(LANES, count * LANES), jnp.bfloat16)
    code = jnp.asarray(np.tile(plan.codes[None], (8, 1)))
    f32, bf16 = jnp.float32, jnp.bfloat16
    n1, n2, messages = len(plan.first), len(plan.second), len(directions)
    dma = pltpu.SemaphoreType.DMA
    vmem = pl.BlockSpec(memory_space=pltpu.VMEM)
    solved, left = pl.pallas_call(
        functools.partial(kernel, plan),
        out_shape=(jax.ShapeDtypeStruct((own, cols), f32),) * 2,
        in_specs=[vmem] * 5,
        out_specs=(vmem, vmem),
        scratch_shapes=[
            pltpu.VMEM((plan.halo_all + ROWS, cols + LANES), f32),
            pltpu.VMEM((plan.halo_all, cols + LANES), f32),
            pltpu.VMEM((ITERS - 1, plan.halo_all + ROWS, cols), f32),
            pltpu.VMEM((ITERS - 1, plan.halo_all, cols), f32),
            pltpu.VMEM((plan.ext, cols), f32),
            pltpu.VMEM((plan.ext, cols), f32),
            pltpu.VMEM((own, plan.ext), bf16),
            pltpu.VMEM((own, plan.ext), bf16),
            pltpu.VMEM((ITERS, ROWS, cols), f32),
            pltpu.VMEM((ITERS, n1, ROWS, cols), f32),
            pltpu.VMEM((ITERS, ROWS, cols), f32),
            pltpu.VMEM((ITERS, n2, ROWS, cols), f32),
            dma((ITERS, messages)), dma((ITERS, messages)),
            dma((ITERS, n1)), dma((ITERS, n1)),
            dma((ITERS, n2)), dma((ITERS, n2)),
        ],
        compiler_params=pltpu.CompilerParams(
            collective_id=0, has_side_effects=True, vmem_limit_bytes=60 * 1024 * 1024
        ),
    )(right_side.reshape(own, cols), lines, column_shift[None], code, spread)
    return solved.reshape(right_side.shape), left.reshape(right_side.shape)


def solution(mesh):
    field = P("gx", "gy", "gz", None, None)
    placed = (
        field,
        P(None, None, None, "gx", "gy", "gz"),
        P(None, "gx", "gy", "gz"),
        P(None, None, "gx", "gy", "gz"),
        P(None, "gx", "gy", "gz"),
        P(),
    )
    return jax.shard_map(
        functools.partial(per_device, tuple(mesh.shape[name] for name in AXES)),
        mesh=mesh,
        in_specs=placed,
        out_specs=(field, field),
        check_vma=False,
    )
```

time: 355 us -> 68.5 us (0.19); the launches traced: 349 us -> 68.2 us
  other arithmetic: 159 us -> 2.92 us
  blocking collectives: 118 us -> 0 us
  Pallas kernels: 0 us -> 55.8 us
  starting transfers between devices: 37.1 us -> 0 us
  waiting for transfers between devices: 17.9 us -> 0 us
  local copies, waits for them, and re-layouts: 13.9 us -> 8.73 us
    add x171 -> x0, other arithmetic: 143 us -> none  [the longest x162 117 us: block_apply(): total = term if total is None else total + term]
    psum x3 -> x0, blocking collectives: 118 us -> none  [two_products(): lax.psum((jnp.sum(residual * residual, axis=(0, 1, 2, 3)), jnp.sum(residu...]
    pallas_call x0 -> x1, Pallas kernels: none -> 55.8 us  [per_device(): pl.pallas_call(functools.partial(kernel, plan), out_shape=(jax.ShapeDtype...]
    ppermute x30 -> x0, starting transfers between devices: 37.1 us -> none  [the longest x18 20.5 us: shifted(): lax.ppermute(value, axis, [(i, (i + by) % peers) for i in range(peers)])]
    ppermute x30 -> x0, waiting for transfers between devices: 17.9 us -> none  [the longest x6 9.28 us: extended_2(): lax.ppermute(head, axis, [((i + 1) % count, i) for i in range(count)])]
    reduce_sum x3 -> x0, other arithmetic: 11.9 us -> none  [two_products(): jnp.sum(residual * image, axis=(0, 1, 2, 3))]
    slice x14 -> x0, local copies, waits for them, and re-layouts: 10.1 us -> none  [the longest x1 8.42 us: operate(): coupled[bond_index]]
    reshape x0 -> x7, local copies, waits for them, and re-layouts: none -> 7.43 us  [the longest x2 3.45 us: per_device(): return (solved.reshape(right_side.shape), left.reshape(right_side.shape))]
  transfers between devices with their start and end apart: 30 -> 0, of which waited for: 12 -> 0; matrix products, arithmetic and copies ran while one was open for 33% -> 0% of each run, Pallas kernels for 0% -> 0%
where the time goes in v1:
time: 68.5 us; the launch traced here: 68.2 us
  Pallas kernels  55.8 us (81%)
  local copies, waits for them, and re-layouts  8.73 us (13%)
  other arithmetic  2.92 us (4%)
  between operations  0.71 us (1%)
    pallas_call x1, Pallas kernels, per_device(): pl.pallas_call(functools.partial(kernel, plan), out_shape=(jax.ShapeDtype...  55.8 us
    reshape x2, local copies, waits for them, and re-layouts, per_device(): return (solved.reshape(right_side.shape), left.reshape(right_side.shape))  3.45 us
    reshape x2, local copies, waits for them, and re-layouts, per_device(): lines = jnp.transpose(lines, (3, 1, 0, 2)).reshape(own, (bonds + 1) * orb)  2.9 us

profile of v1, /device:TPU:0, one launch (start us, length us, event | category | flops | bytes accessed | tf_op | source)
XLA Modules:
  0.0 68.2 jit_solution(15500254027024300252)
XLA Ops:
  0.6 0.8 %convert_element_type.4 = f32[13,4,4,4]{0,3,2,1:T(4,128)S(1)} convert(s32[13,4,4,4]{0,3,2,1:T(4,128)} %param.10) | non-fusion elementwise | flops 832 | bytes 6656 | tf_op jit(solution)/shard_map/convert_element_type | solution.py:251
  1.4 1.1 %broadcast_multiply_fusion = f32[13,4,4,4,2,8]{0,5,4,3,2,1:T(8,128)S(1)} fusion(f32[13,4,4,4,2,8]{0,5,4,3,2,1:T(8,128)} %bitcast.15, f32[13,4,2,8]{0,3,2,1:T(8,128)S(1)} %bitcast.16), kind=kLoop, calls=%fused_computation | loop fusion | flops 13312 | bytes 109824 | tf_op jit(solution)/shard_map/mul | solution.py:251
  2.5 0.2 copy.31
  2.7 1.0 %fusion = f32[4,4,4,4,4]{4,3,2,1,0:T(4,128)S(1)} fusion(f32[4,4,4,4,4]{4,3,2,1,0:T(4,128)} %param.11), kind=kLoop, calls=%fused_computation.2 | loop fusion | flops 2048 | bytes 8192 | tf_op jit(solution)/shard_map/mul | solution.py:252
  3.7 0.2 concatenate.14
  4.0 0.0 copy-start.1
  4.0 2.0 %copy.38 = f32[64,4,14,4]{3,2,1,0:T(8,128)S(1)} copy(f32[64,4,14,4]{0,3,1,2:T(4,128)S(1)} %maximum_bitcast_fusion) | data formatting | bytes 114688 | tf_op jit(solution)/shard_map/reshape | solution.py:255
  6.0 0.0 copy-start
  6.0 0.9 %reshape.34 = f32[256,56]{1,0:T(8,128)S(1)} reshape(f32[64,4,14,4]{3,2,1,0:T(8,128)S(1)} %copy.38) | data formatting | bytes 114688 | tf_op jit(solution)/shard_map/reshape | solution.py:255
  6.9 0.0 copy-done.1
  6.9 0.2 copy.39
  7.1 0.1 reshape.35
  7.2 0.9 %concatenate.16.w_ref = f32[256,128]{1,0:T(8,128)} concatenate(f32[256,56]{1,0:T(8,128)S(1)} %reshape.34, f32[256,1]{1,0:T(8,128)S(1)} %reshape.35, f32[256,7]{1,0:T(8,128)S(1)} %broadcast_in_dim.8, f32[256,56]{1,0:T(8,128)S(1)} %reshape.34, f32[256,1]{1,0:T(8,128)S(1)} %reshape.35, f32[256,7]{1,0:T(8,128)S(1)} %broadcast_in_dim.8), dimensions={1} | concatenate | bytes 262144 | tf_op jit(solution)/shard_map/concatenate | solution.py:258
  8.1 0.0 copy-done
  8.1 0.8 %reshape.28.rs_ref = f32[256,256]{1,0:T(8,128)} reshape(f32[4,4,4,4,256]{4,3,2,1,0:T(4,128)S(1)} %copy-done) | data formatting | bytes 524288 | tf_op jit(solution)/shard_map/reshape | solution.py:296
  8.9 55.8 %shard_map.95 = (f32[256,256]{1,0:T(8,128)}, f32[256,256]{1,0:T(8,128)}) custom-call(f32[256,256]{1,0:T(8,128)} %reshape.28.rs_ref, f32[256,128]{1,0:T(8,128)} %concatenate.16.w_ref, f32[1,256]{1,0:T(1,128)} %bitcast.18, f32[8,896]{1,0:T(8,128)} %constant.9.clone.code_ref, bf16[128,1792]{1,0:T(8,128)(2,1)} %constant.8.clone.spread_ref), custom_call_target="tpu_custom_call" | custom-call | tf_op jit(solution)/shard_map/pallas_call | solution.py:271
  64.7 1.7 %reshape.32 = f32[4,4,4,4,256]{4,3,2,1,0:T(4,128)} reshape(f32[256,256]{1,0:T(8,128)} %get-tuple-element.4) | data formatting | bytes 524288 | tf_op jit(solution)/shard_map/reshape | solution.py:297
  66.4 1.7 %reshape.33 = f32[4,4,4,4,256]{4,3,2,1,0:T(4,128)} reshape(f32[256,256]{1,0:T(8,128)} %get-tuple-element.5) | data formatting | bytes 524288 | tf_op jit(solution)/shard_map/reshape | solution.py:297
  (2 shorter events, 0.0 us)
Async XLA Ops:
  4.0 2.9 %copy-start.1 = (f32[4,4,4,4]{3,2,1,0:T(4,128)S(1)}, f32[4,4,4,4]{3,2,1,0:T(4,128)}, u32[]{:S(2)}) copy-start(f32[4,4,4,4]{3,2,1,0:T(4,128)} %param.12) | copy-start | bytes 3076
  6.0 2.1 %copy-start = (f32[4,4,4,4,256]{4,3,2,1,0:T(4,128)S(1)}, f32[4,4,4,4,256]{4,3,2,1,0:T(4,128)}, u32[]{:S(2)}) copy-start(f32[4,4,4,4,256]{4,3,2,1,0:T(4,128)} %param.8) | copy-start | bytes 786436
